TPU v7x, 8 devices: a whole 2x2x1 slice. The times are simulated.
8 devices in a mesh: stage: 2 (over z, y), expert: 4 (over x, core).
Axes of the slice: x: 2, y: 2, z: 1, core: 2. Of those that a mesh axis runs over, the one named last changes fastest.
Arguments:
- x_act: bfloat16 [2, 8192, 2048], P('stage', 'expert')
- route_idx: int32 [2, 8192, 2], P('stage', 'expert')
- route_wts: float32 [2, 8192, 2], P('stage', 'expert')
- w_one: bfloat16 [2, 8, 2048, 768], P('stage', 'expert')
- w_three: bfloat16 [2, 8, 2048, 768], P('stage', 'expert')
- w_two: bfloat16 [2, 8, 768, 2048], P('stage', 'expert')
- dy_act: bfloat16 [2, 8192, 2048], P('stage', 'expert')
Outputs:
- output 1: bfloat16 [2, 8192, 2048], P('stage', 'expert')
- output 2: bfloat16 [2, 8192, 2048], P('stage', 'expert')
- output 3: bfloat16 [2, 8, 2048, 768], P('stage', 'expert')
- output 4: bfloat16 [2, 8, 2048, 768], P('stage', 'expert')
- output 5: bfloat16 [2, 8, 768, 2048], P('stage', 'expert')
All inputs are finite; a program needn't handle non-finite values.
Results may differ from a plain program's by a relative error of at most 0.0123829.
Values are sent between devices in bfloat16 or wider.
A program may use at most 1 GiB of HBM per device.

v0:
```python
import jax
import jax.numpy as jnp
from jax import lax
from jax.sharding import PartitionSpec as P


def slot_tables(idx_blk, first_exp, n_exp, capacity):
    n_slot = idx_blk.shape[0] * idx_blk.shape[1]
    slot_ids = idx_blk.reshape(n_slot) - first_exp
    hit_mat = (slot_ids[:, None] == jnp.arange(n_exp, dtype=jnp.int32)[None, :]).astype(jnp.int32)
    slot_rank = jnp.sum(jnp.cumsum(hit_mat, axis=0) * hit_mat, axis=1) - 1
    is_local = (slot_ids >= 0) & (slot_ids < n_exp)
    buf_pos = jnp.where(is_local, slot_ids * capacity + slot_rank, n_exp * capacity)
    slot_at = jnp.full((n_exp * capacity,), n_slot, jnp.int32).at[buf_pos].set(jnp.arange(n_slot, dtype=jnp.int32), mode='drop')
    return buf_pos, slot_at


def take_rows(row_table, row_ids):
    return jnp.take(row_table, row_ids, axis=0, mode='fill', fill_value=0)


def expert_forward(x_buf, w_in_one, w_in_three, w_out):
    pre_one = jnp.einsum('pecd,edf->pecf', x_buf, w_in_one, preferred_element_type=jnp.float32)
    pre_three = jnp.einsum('pecd,edf->pecf', x_buf, w_in_three, preferred_element_type=jnp.float32)
    hidden = (pre_one * jax.nn.sigmoid(pre_one) * pre_three).astype(jnp.bfloat16)
    return jnp.einsum('pecf,efd->pecd', hidden, w_out, preferred_element_type=jnp.float32).astype(jnp.bfloat16)


def expert_backward(x_buf, d_buf, w_in_one, w_in_three, w_out):
    pre_one = jnp.einsum('pecd,edf->pecf', x_buf, w_in_one, preferred_element_type=jnp.float32)
    pre_three = jnp.einsum('pecd,edf->pecf', x_buf, w_in_three, preferred_element_type=jnp.float32)
    sig_one = jax.nn.sigmoid(pre_one)
    act_one = pre_one * sig_one
    hidden = (act_one * pre_three).astype(jnp.bfloat16)
    d_hidden = jnp.einsum('pecd,efd->pecf', d_buf, w_out, preferred_element_type=jnp.float32).astype(jnp.bfloat16).astype(jnp.float32)
    d_three = (d_hidden * act_one).astype(jnp.bfloat16)
    d_one = (d_hidden * pre_three * sig_one * (1.0 + pre_one * (1.0 - sig_one))).astype(jnp.bfloat16)
    dx_buf = (jnp.einsum('pecf,edf->pecd', d_one, w_in_one, preferred_element_type=jnp.float32) + jnp.einsum('pecf,edf->pecd', d_three, w_in_three, preferred_element_type=jnp.float32)).astype(jnp.bfloat16)
    g_one = jnp.einsum('pecd,pecf->edf', x_buf, d_one, preferred_element_type=jnp.float32).astype(jnp.bfloat16)
    g_three = jnp.einsum('pecd,pecf->edf', x_buf, d_three, preferred_element_type=jnp.float32).astype(jnp.bfloat16)
    g_two = jnp.einsum('pecf,pecd->efd', hidden, d_buf, preferred_element_type=jnp.float32).astype(jnp.bfloat16)
    return dx_buf, g_one, g_three, g_two


def solution(mesh):
    n_stage = mesh.shape['stage']
    n_dev = mesh.shape['expert']
    to_next = [(stage_idx, (stage_idx + 1) % n_stage) for stage_idx in range(n_stage)]
    to_prev = [((stage_idx + 1) % n_stage, stage_idx) for stage_idx in range(n_stage)]
    tok_spec = P('stage', 'expert', None)
    w_spec = P('stage', 'expert', None, None)

    def moe_layer(x_act, route_idx, route_wts, w_one, w_three, w_two, dy_act):
        x_src = x_act[0]
        n_tok, model_dim = x_src.shape
        top_k = route_idx.shape[2]
        n_local = w_one.shape[1]
        n_exp = n_local * n_dev
        capacity = 2 * n_tok * top_k // n_exp - 1
        w_in_one, w_in_three, w_out = w_one[0], w_three[0], w_two[0]

        x_dst = lax.ppermute(x_src, 'stage', to_next)
        idx_dst = lax.ppermute(route_idx[0], 'stage', to_next)
        wts_dst = lax.ppermute(route_wts[0], 'stage', to_next)
        buf_pos, slot_at = slot_tables(idx_dst, 0, n_exp, capacity)

        def dispatch(row_src, row_ids):
            send_buf = take_rows(row_src, row_ids).reshape(n_dev, n_local, capacity, model_dim)
            return lax.all_to_all(send_buf, 'expert', 0, 0)

        def combine(buf_rows):
            back_buf = lax.all_to_all(buf_rows, 'expert', 0, 0).reshape(n_exp * capacity, model_dim)
            return take_rows(back_buf, buf_pos).reshape(n_tok, top_k, model_dim)

        out_slot = combine(expert_forward(dispatch(x_dst, slot_at // top_k), w_in_one, w_in_three, w_out))
        y_dst = jnp.sum(wts_dst[:, :, None] * out_slot.astype(jnp.float32), axis=1).astype(jnp.bfloat16)

        x_again, y_dst = lax.optimization_barrier((x_src, y_dst))
        x_dst = lax.ppermute(x_again, 'stage', to_next)
        d_slot = (wts_dst[:, :, None] * dy_act[0][:, None, :].astype(jnp.float32)).astype(jnp.bfloat16).reshape(n_tok * top_k, model_dim)
        dx_buf, g_one, g_three, g_two = expert_backward(dispatch(x_dst, slot_at // top_k), dispatch(d_slot, slot_at), w_in_one, w_in_three, w_out)
        dx_slot = combine(dx_buf)
        dx_dst = jnp.sum(dx_slot.astype(jnp.float32), axis=1).astype(jnp.bfloat16)
        dx_src = lax.ppermute(dx_dst, 'stage', to_prev)
        return y_dst[None], dx_src[None], g_one[None], g_three[None], g_two[None]

    return jax.shard_map(moe_layer, mesh=mesh, in_specs=(tok_spec, tok_spec, tok_spec, w_spec, w_spec, w_spec, tok_spec), out_specs=(tok_spec, tok_spec, w_spec, w_spec, w_spec), check_vma=False)
```

profile of v0, /device:TPU:0, one launch (start us, length us, event | category | flops | bytes accessed | tf_op | source)
XLA Modules:
  0.0 3438.9 jit_solution(2888706820705303422)
XLA Ops:
  0.6 3.4 collective-permute-start.1
  4.1 180.8 %collective-permute-done.2 = s32[2048,2]{0,1:T(2,128)S(1)} collective-permute-done((s32[2048,2]{0,1:T(2,128)}, s32[2048,2]{0,1:T(2,128)S(1)}, u32[]{:S(2)}, u32[]{:S(2)}) %collective-permute-start.2) | collective-permute-done | bytes 16416 | tf_op jit(solution)/shard_map/ppermute | solution.py:63
  186.7 0.7 and.35
  187.4 2.3 reduce-window.6
  190.6 0.6 mul.79
  191.4 0.6 broadcast_clamp_fusion
  192.1 15.5 scatter_custom_fusion
  207.7 0.6 compare_and_fusion
  208.4 66.2 %gather_fusion.1 = bf16[8184,2048]{1,0:T(8,128)(2,1)} fusion(bf16[2048,2048]{1,0:T(8,128)(2,1)} %collective-permute-done.1, s32[8192]{0:T(1024)S(1)} %pad_clamp_fusion.1), kind=kCustom, calls=%fused_computation.clone | custom fusion | bytes 67076064 | tf_op jit(solution)/shard_map/jit(_take)/gather | solution.py:19
  274.6 22.9 broadcast_select_fusion.2
  297.5 32.9 reshape.144
  330.4 56.5 %copy.36 = bf16[4,2,1023,2048]{3,1,2,0:T(2,128)(2,1)} copy(bf16[4,2,1023,2048]{3,2,1,0:T(8,128)(2,1)} %reshape.144) | data formatting | bytes 67043328 | tf_op jit(solution)/shard_map/reshape | solution.py:68
  386.9 380.1 %all_to_all.25 = bf16[4,2,1023,2048]{3,1,2,0:T(2,128)(2,1)} all-to-all(bf16[4,2,1023,2048]{3,1,2,0:T(2,128)(2,1)} %copy.36), channel_id=1, replica_groups=mesh['stage'=2,'expert'=4] {'expert'}, dimensions={0} | all-to-all | bytes 67043328 | tf_op jit(solution)/shard_map/all_to_all | solution.py:69
  767.0 44.2 %fusion.4 = f32[2,4,1023,768]{3,2,1,0:T(8,128)} fusion(bf16[4,2,1023,2048]{3,1,2,0:T(2,128)(2,1)} %all_to_all.25, bf16[1,2,2048,768]{3,2,1,0:T(8,128)(2,1)S(1)} %bitcast.181), kind=kOutput, calls=%fused_computation.17 | convolution fusion | flops 25744637952 | bytes 64954368 | tf_op jit(solution)/shard_map/pecd,edf->pecf/dot_general | solution.py:24
  811.2 49.4 %fusion.83 = bf16[4,2,1023,768]{3,2,0,1:T(8,128)(2,1)} fusion(f32[2,4,1023,768]{3,2,1,0:T(8,128)} %fusion.4, bf16[1,2,2048,768]{3,2,1,0:T(8,128)(2,1)} %param.14, bf16[4,2,1023,2048]{3,1,2,0:T(2,128)(2,1)} %all_to_all.25), kind=kOutput, calls=%fused_computation.37.clone.clone.1 | convolution fusion | flops 25782349824 | bytes 77524992 | tf_op jit(solution)/shard_map/pecd,edf->pecf/dot_general | solution.py:23
  860.7 33.9 convert_bitcast_fusion
  894.6 56.2 %copy.39 = bf16[4,2,1023,2048]{3,1,2,0:T(2,128)(2,1)} copy(bf16[4,2,1023,2048]{3,2,0,1:T(8,128)(2,1)} %convert_bitcast_fusion) | data formatting | bytes 67043328 | tf_op jit(solution)/shard_map/convert_element_type | solution.py:26
  950.8 9.9 all-to-all-start.1
  960.8 1.8 collective-permute-start
  962.5 11.3 bitcast_convert_fusion.3
  973.8 21.6 mul.88
  995.4 39.8 %mul.89 = f32[4096,2048]{1,0:T(8,128)} reshape(f32[2048,2,2048]{2,1,0:T(2,128)} %mul.88) | data formatting | bytes 67108864 | tf_op jit(solution)/shard_map/mul | solution.py:80
  1036.2 17.9 multiply_convert_fusion
  1054.1 69.8 %gather_fusion = bf16[8184,2048]{1,0:T(8,128)(2,1)} fusion(bf16[4096,2048]{1,0:T(8,128)(2,1)} %multiply_convert_fusion, s32[8192]{0:T(1024)S(1)} %pad_clamp_fusion), kind=kCustom, calls=%fused_computation.4 | custom fusion | bytes 67076064 | tf_op jit(solution)/shard_map/jit(_take)/gather | solution.py:19
  1124.0 32.7 gather.13
  1156.7 23.0 broadcast_select_fusion
  1179.7 55.7 %copy.42 = bf16[4,2,1023,2048]{3,1,2,0:T(2,128)(2,1)} copy(bf16[4,2,1023,2048]{3,2,1,0:T(8,128)(2,1)} %broadcast_select_fusion) | data formatting | bytes 67043328 | tf_op jit(solution)/shard_map/jit(_take)/select_n | solution.py:19
  1235.4 87.5 %all-to-all-done.1 = bf16[4,2,1023,2048]{3,1,2,0:T(2,128)(2,1)} async-done(((bf16[4,2,1023,2048]{3,1,2,0:T(2,128)(2,1)}), bf16[4,2,1023,2048]{3,1,2,0:T(2,128)(2,1)}, u32[]{:S(2)}, u32[]{:S(2)}) %all-to-all-start.1) | async-done | bytes 33521696 | tf_op jit(solution)/shard_map/all_to_all | solution.py:72
  1322.9 9.9 all-to-all-start.2
  1332.8 23.1 copy.40
  1355.9 32.7 reshape.145
  1388.7 96.0 %gather_fusion.2 = bf16[4096,2048]{1,0:T(8,128)(2,1)} fusion(bf16[8184,2048]{1,0:T(8,128)(2,1)} %reshape.145, s32[4096]{0:T(1024)S(1)} %copy-done.8), kind=kCustom, calls=%fused_computation.1.clone | custom fusion | bytes 33570816 | tf_op jit(solution)/shard_map/jit(_take)/gather | solution.py:19
  1484.7 18.7 select_convert_fusion
  1503.4 39.1 %reshape.149 = f32[2048,2,2048]{2,1,0:T(2,128)} reshape(f32[4096,2048]{1,0:T(8,128)} %select_convert_fusion) | data formatting | bytes 67108864 | tf_op jit(solution)/shard_map/convert_element_type | solution.py:76
  1542.4 54.8 %multiply_reduce_fusion = bf16[2048,2048]{1,0:T(8,128)(2,1)} fusion(f32[2048,2,2048]{2,1,0:T(2,128)} %reshape.149, f32[2048,2]{1,0:T(8,128)S(1)} %copy-done.1), kind=kLoop, calls=%fused_computation.8 | loop fusion | flops 12582912 | bytes 41959424 | tf_op jit(solution)/shard_map/reduce_sum | solution.py:76
  1597.3 1.7 collective-permute-start.3
  1599.0 181.1 %collective-permute-done.3 = bf16[2048,2048]{1,0:T(8,128)(2,1)} collective-permute-done((bf16[2048,2048]{1,0:T(8,128)(2,1)}, bf16[2048,2048]{1,0:T(8,128)(2,1)}, u32[]{:S(2)}, u32[]{:S(2)}) %collective-permute-start.3) | collective-permute-done | bytes 8388640 | tf_op jit(solution)/shard_map/ppermute | solution.py:79
  1780.1 65.9 %gather_fusion.3 = bf16[8184,2048]{1,0:T(8,128)(2,1)} fusion(bf16[2048,2048]{1,0:T(8,128)(2,1)} %collective-permute-done.3, s32[8192]{0:T(1024)S(1)} %copy-done.5), kind=kCustom, calls=%fused_computation.2.clone | custom fusion | bytes 67076064 | tf_op jit(solution)/shard_map/jit(_take)/gather | solution.py:19
  1846.0 23.3 broadcast_select_fusion.1
  1869.3 32.7 reshape.146
  1902.0 55.7 %copy.44 = bf16[4,2,1023,2048]{3,1,2,0:T(2,128)(2,1)} copy(bf16[4,2,1023,2048]{3,2,1,0:T(8,128)(2,1)} %reshape.146) | data formatting | bytes 67043328 | tf_op jit(solution)/shard_map/reshape | solution.py:68
  1957.7 9.9 all-to-all-start.3
  1967.6 46.2 %fusion.25 = bf16[2,4,1023,768]{3,2,1,0:T(8,128)(2,1)} fusion(bf16[4,2,1023,2048]{3,1,2,0:T(2,128)(2,1)} %all-to-all-done.2, bf16[1,2,768,2048]{3,2,1,0:T(8,128)(2,1)} %param.16), kind=kOutput, calls=%fused_computation.51 | convolution fusion | flops 25750923264 | bytes 52383744 | tf_op jit(solution)/shard_map/pecd,efd->pecf/dot_general | solution.py:35
  2013.8 315.9 %all-to-all-done.3 = bf16[4,2,1023,2048]{3,1,2,0:T(2,128)(2,1)} async-done(((bf16[4,2,1023,2048]{3,1,2,0:T(2,128)(2,1)}), bf16[4,2,1023,2048]{3,1,2,0:T(2,128)(2,1)}, u32[]{:S(2)}, u32[]{:S(2)}) %all-to-all-start.3) | async-done | bytes 33521696 | tf_op jit(solution)/shard_map/all_to_all | solution.py:69
  2329.7 81.1 %copy.49 = bf16[4,2,1023,2048]{2,3,0,1:T(8,128)(2,1)} copy(bf16[4,2,1023,2048]{3,1,2,0:T(2,128)(2,1)} %all-to-all-done.3) | data formatting | bytes 67043328 | tf_op jit(solution)/shard_map/all_to_all | solution.py:69
  2410.8 35.6 %fusion.37 = f32[2,4,1023,768]{3,2,1,0:T(8,128)} fusion(bf16[4,2,1023,2048]{2,3,0,1:T(8,128)(2,1)} %copy.49, bf16[1,2,2048,768]{3,2,1,0:T(8,128)(2,1)} %param.15), kind=kOutput, calls=%fused_computation.61 | convolution fusion | flops 25744637952 | bytes 64954368 | tf_op jit(solution)/shard_map/pecd,edf->pecf/dot_general | solution.py:31
  2446.3 46.1 %fusion.13 = (bf16[4,2,1023,768]{3,2,0,1:T(8,128)(2,1)}, f32[2,4,1023,768]{3,2,1,0:T(8,128)}) fusion(f32[2,4,1023,768]{3,2,1,0:T(8,128)} %fusion.37, bf16[2,4,1023,768]{3,2,1,0:T(8,128)(2,1)} %fusion.25, bf16[4,2,1023,2048]{2,3,0,1:T(8,128)(2,1)} %copy.49, bf16[1,2,2048,768]{3,2,1,0:T(8,128)(2,1)} %param.14), kind=kOutput, calls=%fused_computation.29 | convolution fusion | flops 25813776384 | bytes 115236864 | tf_op jit(solution)/shard_map/pecd,edf->pecf/dot_general | solution.py:30
  2492.4 36.8 %fusion.31 = f32[2,4,1023,2048]{3,2,1,0:T(8,128)} fusion(bf16[4,2,1023,768]{3,2,0,1:T(8,128)(2,1)} %get-tuple-element.16, bf16[1,2,2048,768]{3,2,1,0:T(8,128)(2,1)} %param.14), kind=kOutput, calls=%fused_computation.55 | convolution fusion | flops 25744637952 | bytes 85905408 | tf_op jit(solution)/shard_map/pecf,edf->pecd/dot_general | solution.py:38
  2529.2 49.9 %fusion.21 = bf16[4,2,1023,2048]{3,2,0,1:T(8,128)(2,1)} fusion(f32[2,4,1023,2048]{3,2,1,0:T(8,128)} %fusion.31, bf16[1,2,2048,768]{3,2,1,0:T(8,128)(2,1)} %param.15, bf16[2,4,1023,768]{3,2,1,0:T(8,128)(2,1)} %fusion.25, f32[2,4,1023,768]{3,2,1,0:T(8,128)} %get-tuple-element.17), kind=kOutput, calls=%fused_computation.43 | convolution fusion | flops 25822156800 | bytes 144568320 | tf_op jit(solution)/shard_map/pecf,edf->pecd/dot_general | solution.py:38
  2579.1 56.2 %copy.47 = bf16[4,2,1023,2048]{3,1,2,0:T(2,128)(2,1)} copy(bf16[4,2,1023,2048]{3,2,0,1:T(8,128)(2,1)} %fusion.21) | data formatting | bytes 67043328 | tf_op jit(solution)/shard_map/convert_element_type | solution.py:38
  2635.3 9.9 all-to-all-start.4
  2645.2 57.5 %fusion.30 = bf16[1,2,768,2048]{3,2,1,0:T(8,128)(2,1)} fusion(bf16[4,2,1023,2048]{3,1,2,0:T(2,128)(2,1)} %all-to-all-done.2, f32[2,4,1023,768]{3,2,1,0:T(8,128)} %fusion.37, f32[2,4,1023,768]{3,2,1,0:T(8,128)} %get-tuple-element.17), kind=kOutput, calls=%fused_computation.54 | convolution fusion | flops 25785495552 | bytes 90095616 | tf_op jit(solution)/shard_map/pecf,pecd->efd/dot_general | solution.py:41
  2702.7 304.6 %all-to-all-done.4 = bf16[4,2,1023,2048]{3,1,2,0:T(2,128)(2,1)} async-done(((bf16[4,2,1023,2048]{3,1,2,0:T(2,128)(2,1)}), bf16[4,2,1023,2048]{3,1,2,0:T(2,128)(2,1)}, u32[]{:S(2)}, u32[]{:S(2)}) %all-to-all-start.4) | async-done | bytes 33521696 | tf_op jit(solution)/shard_map/all_to_all | solution.py:72
  3007.3 23.3 copy.48
  3030.6 32.7 reshape.147
  3063.4 95.9 %gather_fusion.4 = bf16[4096,2048]{1,0:T(8,128)(2,1)} fusion(bf16[8184,2048]{1,0:T(8,128)(2,1)} %reshape.147, s32[4096]{0:T(1024)S(1)} %copy-done.9), kind=kCustom, calls=%fused_computation.3.clone | custom fusion | bytes 33570816 | tf_op jit(solution)/shard_map/jit(_take)/gather | solution.py:19
  3159.3 14.9 broadcast_select_fusion.3
  3174.1 27.1 reshape.148
  3201.2 47.0 %reduce_sum.32 = bf16[2048,2048]{1,0:T(8,128)(2,1)} reduce(bf16[2048,2,2048]{2,1,0:T(2,128)(2,1)} %reshape.148, bf16[]{:T(256)} %constant.71.clone.1), dimensions={1}, to_apply=%region_5.8 | reduce | flops 4194304 | bytes 25165826 | tf_op jit(solution)/shard_map/reduce_sum | solution.py:83
  3248.2 1.7 collective-permute-start.4
  3249.9 34.7 %fusion.28 = bf16[1,2,2048,768]{3,2,1,0:T(8,128)(2,1)} fusion(bf16[4,2,1023,2048]{2,3,0,1:T(8,128)(2,1)} %copy.49, bf16[4,2,1023,768]{3,2,0,1:T(8,128)(2,1)} %get-tuple-element.16), kind=kOutput, calls=%fused_computation.52 | convolution fusion | flops 25747783680 | bytes 52383744 | tf_op jit(solution)/shard_map/pecd,pecf->edf/dot_general | solution.py:39
  3284.7 36.4 %fusion.29 = bf16[1,2,2048,768]{3,2,1,0:T(8,128)(2,1)} fusion(bf16[4,2,1023,2048]{2,3,0,1:T(8,128)(2,1)} %copy.49, bf16[2,4,1023,768]{3,2,1,0:T(8,128)(2,1)} %fusion.25, f32[2,4,1023,768]{3,2,1,0:T(8,128)} %get-tuple-element.17), kind=kOutput, calls=%fused_computation.53 | convolution fusion | flops 25791780864 | bytes 77524992 | tf_op jit(solution)/shard_map/pecd,pecf->edf/dot_general | solution.py:40
  3321.1 109.1 %collective-permute-done.4 = bf16[2048,2048]{1,0:T(8,128)(2,1)} collective-permute-done((bf16[2048,2048]{1,0:T(8,128)(2,1)}, bf16[2048,2048]{1,0:T(8,128)(2,1)}, u32[]{:S(2)}, u32[]{:S(2)}) %collective-permute-start.4) | collective-permute-done | bytes 8388640 | tf_op jit(solution)/shard_map/ppermute | solution.py:84
  3430.2 8.4 copy.82
  (66 shorter events, 4.0 us)
Async XLA Ops:
  0.6 207.7 %collective-permute-start.1 = (bf16[2048,2048]{1,0:T(8,128)(2,1)}, bf16[2048,2048]{1,0:T(8,128)(2,1)}, u32[]{:S(2)}, u32[]{:S(2)}) collective-permute-start(bf16[2048,2048]{1,0:T(8,128)(2,1)} %bitcast.178), channel_id=1, source_target_pairs={{0,4},{4,0},{1,5},{5,1},{2,6},{6,2},{3,7},{7,3}} | collective-permute-start | bytes 25165832 | tf_op jit(solution)/shard_map/ppermute | solution.py:62
  4.0 180.8 %collective-permute-start.2 = (s32[2048,2]{0,1:T(2,128)}, s32[2048,2]{0,1:T(2,128)S(1)}, u32[]{:S(2)}, u32[]{:S(2)}) collective-permute-start(s32[2048,2]{0,1:T(2,128)} %bitcast.182), channel_id=1, source_target_pairs={{0,4},{4,0},{1,5},{5,1},{2,6},{6,2},{3,7},{7,3}} | collective-permute-start | bytes 49160 | tf_op jit(solution)/shard_map/ppermute | solution.py:63
  185.7 88.9 %copy-start.6 = (s32[4096]{0:T(1024)}, s32[4096]{0:T(1024)S(1)}, u32[]{:S(2)}) copy-start(s32[4096]{0:T(1024)S(1)} %eq.25) | copy-start | bytes 49156
  191.4 0.7 copy-start.10
  207.7 66.9 %copy-start.2 = (s32[8184]{0:T(1024)}, s32[8184]{0:T(1024)S(1)}, u32[]{:S(2)}) copy-start(s32[8184]{0:T(1024)S(1)} %scatter_custom_fusion) | copy-start | bytes 98212
  208.3 66.3 %copy-start.12 = (pred[8184]{0:T(1024)(128)(4,1)}, pred[8184]{0:T(1024)(128)(4,1)S(1)}, u32[]{:S(2)}) copy-start(pred[8184]{0:T(1024)(128)(4,1)S(1)} %get-tuple-element.11) | copy-start | bytes 24556
  208.3 66.2 %copy-start.4 = (s32[8192]{0:T(1024)}, s32[8192]{0:T(1024)S(1)}, u32[]{:S(2)}) copy-start(s32[8192]{0:T(1024)S(1)} %pad_clamp_fusion.1) | copy-start | bytes 98308
  297.5 469.5 %slice-start = ((s8[6291456]{0:T(1024)(128)(4,1)}), s8[2097152]{0:T(1024)(128)(4,1)S(1)}, s32[]{:S(2)}) async-start(s8[6291456]{0:T(1024)(128)(4,1)} %bitcast.180), calls=%async_computation.5 | async-start | bytes 4194304
  330.4 436.6 %slice-start.1 = ((s8[6291456]{0:T(1024)(128)(4,1)}), s8[4194304]{0:T(1024)(128)(4,1)S(1)}, s32[]{:S(2)}) async-start(s8[6291456]{0:T(1024)(128)(4,1)} %bitcast.180), calls=%async_computation.6 | async-start | bytes 8388608
  950.8 9.9 copy-start.17
  950.8 372.1 %all-to-all-start.1 = ((bf16[4,2,1023,2048]{3,1,2,0:T(2,128)(2,1)}), bf16[4,2,1023,2048]{3,1,2,0:T(2,128)(2,1)}, u32[]{:S(2)}, u32[]{:S(2)}) async-start(bf16[4,2,1023,2048]{3,1,2,0:T(2,128)(2,1)} %copy.39), calls=%async_computation.1 | async-start | bytes 67043328 | tf_op jit(solution)/shard_map/all_to_all | solution.py:72
  960.8 74.5 %collective-permute-start = (f32[2048,2]{0,1:T(2,128)S(1)}, f32[2048,2]{0,1:T(2,128)S(1)}, u32[]{:S(2)}, u32[]{:S(2)}) collective-permute-start(f32[2048,2]{0,1:T(2,128)S(1)} %bitcast.183), channel_id=1, source_target_pairs={{0,4},{4,0},{1,5},{5,1},{2,6},{6,2},{3,7},{7,3}} | collective-permute-start | bytes 49160 | tf_op jit(solution)/shard_map/ppermute | solution.py:64
  995.4 40.7 %copy-start.16 = (pred[8184]{0:T(1024)(128)(4,1)S(1)}, pred[8184]{0:T(1024)(128)(4,1)}, u32[]{:S(2)}) copy-start(pred[8184]{0:T(1024)(128)(4,1)} %get-tuple-element.13) | copy-start | bytes 24556
  995.4 40.8 %copy-start.3 = (s32[8184]{0:T(1024)S(1)}, s32[8184]{0:T(1024)}, u32[]{:S(2)}) copy-start(s32[8184]{0:T(1024)} %copy-done.2) | copy-start | bytes 98212
  1035.6 18.5 copy-start
  1235.4 97.4 %copy-start.7 = (s32[4096]{0:T(1024)S(1)}, s32[4096]{0:T(1024)}, u32[]{:S(2)}) copy-start(s32[4096]{0:T(1024)} %copy-done.6) | copy-start | bytes 49156
  1235.4 97.4 %copy-start.11 = (s32[4096]{0:T(1024)S(1)}, s32[4096]{0:T(1024)}, u32[]{:S(2)}) copy-start(s32[4096]{0:T(1024)} %copy-done.10) | copy-start | bytes 49156
  1322.9 634.8 %all-to-all-start.2 = ((bf16[4,2,1023,2048]{3,1,2,0:T(2,128)(2,1)}), bf16[4,2,1023,2048]{3,1,2,0:T(2,128)(2,1)}, u32[]{:S(2)}, u32[]{:S(2)}) async-start(bf16[4,2,1023,2048]{3,1,2,0:T(2,128)(2,1)} %copy.42), calls=%async_computation.2 | async-start | bytes 67043328 | tf_op jit(solution)/shard_map/all_to_all | solution.py:69
  1332.8 151.9 %copy-start.14 = (pred[4096]{0:T(1024)(128)(4,1)}, pred[4096]{0:T(1024)(128)(4,1)S(1)}, u32[]{:S(2)}) copy-start(pred[4096]{0:T(1024)(128)(4,1)S(1)} %compare_and_fusion.3) | copy-start | bytes 12292
  1355.9 32.7 copy-start.8
  1503.4 39.1 %copy-start.1 = (f32[2048,2]{1,0:T(8,128)S(1)}, f32[2048,2]{1,0:T(8,128)}, u32[]{:S(2)}) copy-start(f32[2048,2]{1,0:T(8,128)} %copy-done) | copy-start | bytes 49156
  1542.4 237.7 %copy-start.5 = (s32[8192]{0:T(1024)S(1)}, s32[8192]{0:T(1024)}, u32[]{:S(2)}) copy-start(s32[8192]{0:T(1024)} %copy-done.4) | copy-start | bytes 98308
  1597.3 248.7 %copy-start.13 = (pred[8184]{0:T(1024)(128)(4,1)S(1)}, pred[8184]{0:T(1024)(128)(4,1)}, u32[]{:S(2)}) copy-start(pred[8184]{0:T(1024)(128)(4,1)} %copy-done.12) | copy-start | bytes 24556
  1597.3 182.8 %collective-permute-start.3 = (bf16[2048,2048]{1,0:T(8,128)(2,1)}, bf16[2048,2048]{1,0:T(8,128)(2,1)}, u32[]{:S(2)}, u32[]{:S(2)}) collective-permute-start(bf16[2048,2048]{1,0:T(8,128)(2,1)} %bitcast.179), channel_id=1, source_target_pairs={{0,4},{4,0},{1,5},{5,1},{2,6},{6,2},{3,7},{7,3}} | collective-permute-start | bytes 25165832 | tf_op jit(solution)/shard_map/ppermute | solution.py:79
  1957.7 372.0 %all-to-all-start.3 = ((bf16[4,2,1023,2048]{3,1,2,0:T(2,128)(2,1)}), bf16[4,2,1023,2048]{3,1,2,0:T(2,128)(2,1)}, u32[]{:S(2)}, u32[]{:S(2)}) async-start(bf16[4,2,1023,2048]{3,1,2,0:T(2,128)(2,1)} %copy.44), calls=%async_computation.3 | async-start | bytes 67043328 | tf_op jit(solution)/shard_map/all_to_all | solution.py:69
  2635.3 372.0 %all-to-all-start.4 = ((bf16[4,2,1023,2048]{3,1,2,0:T(2,128)(2,1)}), bf16[4,2,1023,2048]{3,1,2,0:T(2,128)(2,1)}, u32[]{:S(2)}, u32[]{:S(2)}) async-start(bf16[4,2,1023,2048]{3,1,2,0:T(2,128)(2,1)} %copy.47), calls=%async_computation.4 | async-start | bytes 67043328 | tf_op jit(solution)/shard_map/all_to_all | solution.py:72
  3030.6 32.7 copy-start.9
  3063.3 95.9 %copy-start.15 = (pred[4096]{0:T(1024)(128)(4,1)S(1)}, pred[4096]{0:T(1024)(128)(4,1)}, u32[]{:S(2)}) copy-start(pred[4096]{0:T(1024)(128)(4,1)} %copy-done.14) | copy-start | bytes 12292
  3248.2 182.0 %collective-permute-start.4 = (bf16[2048,2048]{1,0:T(8,128)(2,1)}, bf16[2048,2048]{1,0:T(8,128)(2,1)}, u32[]{:S(2)}, u32[]{:S(2)}) collective-permute-start(bf16[2048,2048]{1,0:T(8,128)(2,1)} %reduce_sum.32), channel_id=1, source_target_pairs={{4,0},{0,4},{5,1},{1,5},{6,2},{2,6},{7,3},{3,7}} | collective-permute-start | bytes 25165832 | tf_op jit(solution)/shard_map/ppermute | solution.py:84
where the time goes:
time: 3450 us; the launch traced here: 3440 us
  waiting for transfers between devices  1180 us (34%)
  local copies, waits for them, and re-layouts  1120 us (32%)
  matrix products  471 us (14%)
  blocking collectives  380 us (11%)
  other arithmetic  238 us (7%)
  starting transfers between devices  48.3 us (1%)
    gather x6, local copies, waits for them, and re-layouts, take_rows(): return jnp.take(row_table, row_ids, axis=0, mode='fill', fill_value=0)  427 us
    all_to_all x2, waiting for transfers between devices, combine(): lax.all_to_all(buf_rows, 'expert', 0, 0)  392 us
    all_to_all x1, blocking collectives, dispatch(): return lax.all_to_all(send_buf, 'expert', 0, 0)  380 us
    all_to_all x2, waiting for transfers between devices, dispatch(): return lax.all_to_all(send_buf, 'expert', 0, 0)  316 us
    ppermute x1, waiting for transfers between devices, moe_layer(): x_dst = lax.ppermute(x_again, 'stage', to_next)  181 us
    ppermute x1, waiting for transfers between devices, moe_layer(): idx_dst = lax.ppermute(route_idx[0], 'stage', to_next)  181 us
    reshape x4, local copies, waits for them, and re-layouts, dispatch(): take_rows(row_src, row_ids).reshape(n_dev, n_local, capacity, model_dim)  178 us
    ppermute x1, waiting for transfers between devices, moe_layer(): dx_src = lax.ppermute(dx_dst, 'stage', to_prev)  109 us
  transfers between devices with their start and end apart: 9, of which 6 were waited for; matrix products, arithmetic and copies ran while one was open for 27% of the time, Pallas kernels for 0%

commit v1 on v0

v1 whole, which is shorter than its diff:
```python
import functools

import jax
import jax.numpy as jnp
from jax import lax
from jax.experimental import pallas as pl
from jax.experimental.pallas import tpu as pltpu
from jax.sharding import PartitionSpec as P


TILE = 256
LANES = 128
VMEM_BYTES = 60 * 1024 * 1024
NT = (((1,), (1,)), ((), ()))
TN = (((0,), (0,)), ((), ()))


def dot(lhs, rhs):
    return jnp.dot(lhs, rhs, preferred_element_type=jnp.float32)


def dot_nt(lhs, rhs):
    return lax.dot_general(lhs, rhs, NT, preferred_element_type=jnp.float32)


def dot_tn(lhs, rhs):
    return lax.dot_general(lhs, rhs, TN, preferred_element_type=jnp.float32)


def gate_cols(gates, pos):
    lane = lax.broadcasted_iota(jnp.int32, gates.shape, 1)
    g_cur = jnp.sum(jnp.where(lane == pos, gates, 0.0), axis=1, keepdims=True)
    g_prev = jnp.sum(jnp.where(lane < pos, gates, 0.0), axis=1, keepdims=True)
    return g_cur, g_prev


def weight_stream(groups, bufs, sems):
    n_local = groups[0][0].shape[0]

    def start(pos, slot):
        for grp in range(len(groups)):
            @pl.when(pos // n_local == grp)
            def _():
                for mat in range(3):
                    pltpu.make_async_copy(groups[grp][mat].at[pos % n_local], bufs[mat].at[slot], sems.at[slot, mat]).start()

    def wait(slot):
        for mat in range(3):
            pltpu.make_async_copy(groups[0][mat].at[0], bufs[mat].at[slot], sems.at[slot, mat]).wait()

    return start, wait


def fwd_kernel(n_grp, act_ref, gate_ref, x_ref, *refs):
    w_refs, (y_ref, b_one, b_three, b_two, sems) = refs[:3 * n_grp], refs[3 * n_grp:]
    groups = [w_refs[3 * k:3 * k + 3] for k in range(n_grp)]
    n_pos = n_grp * groups[0][0].shape[0]
    n_tile = x_ref.shape[0] // TILE
    start, wait = weight_stream(groups, (b_one, b_three, b_two), sems)
    start(0, 0)
    y_ref[...] = jnp.zeros_like(y_ref)

    def expert(pos, _):
        slot = lax.rem(pos, 2)
        wait(slot)

        @pl.when(pos + 1 < n_pos)
        def _():
            start(pos + 1, 1 - slot)

        def tile(m, _):
            @pl.when(act_ref[pos * n_tile + m] > 0)
            def _():
                rows = pl.ds(pl.multiple_of(m * TILE, TILE), TILE)
                x = x_ref[rows, :]
                pre_one = dot(x, b_one[slot])
                pre_three = dot(x, b_three[slot])
                hidden = (pre_one * jax.nn.sigmoid(pre_one) * pre_three).astype(jnp.bfloat16)
                out = dot(hidden, b_two[slot]).astype(jnp.bfloat16)
                g_cur, g_prev = gate_cols(gate_ref[rows, :], pos)
                acc = y_ref[rows, :]
                both = (g_prev * acc.astype(jnp.float32) + g_cur * out.astype(jnp.float32)).astype(jnp.bfloat16)
                y_ref[rows, :] = jnp.where(g_cur > 0, jnp.where(g_prev > 0, both, out), acc)
            return 0

        return lax.fori_loop(0, n_tile, tile, 0)

    lax.fori_loop(0, n_pos, expert, 0)


def hidden_grads(x, d_out, w_in_one, w_in_three, w_out):
    pre_one = dot(x, w_in_one)
    pre_three = dot(x, w_in_three)
    d_hidden = dot_nt(d_out, w_out).astype(jnp.bfloat16).astype(jnp.float32)
    sig_one = jax.nn.sigmoid(pre_one)
    act_one = pre_one * sig_one
    d_three = d_hidden * act_one
    d_one = d_hidden * pre_three * sig_one * (1.0 + pre_one * (1.0 - sig_one))
    return act_one * pre_three, d_one, d_three


def dx_kernel(n_grp, act_ref, gate_ref, x_ref, dy_ref, *refs):
    w_refs, (dx_ref, b_one, b_three, b_two, sems) = refs[:3 * n_grp], refs[3 * n_grp:]
    groups = [w_refs[3 * k:3 * k + 3] for k in range(n_grp)]
    n_pos = n_grp * groups[0][0].shape[0]
    n_tile = x_ref.shape[0] // TILE
    start, wait = weight_stream(groups, (b_one, b_three, b_two), sems)
    start(0, 0)
    dx_ref[...] = jnp.zeros_like(dx_ref)

    def expert(pos, _):
        slot = lax.rem(pos, 2)
        wait(slot)

        @pl.when(pos + 1 < n_pos)
        def _():
            start(pos + 1, 1 - slot)

        def tile(m, _):
            @pl.when(act_ref[pos * n_tile + m] > 0)
            def _():
                rows = pl.ds(pl.multiple_of(m * TILE, TILE), TILE)
                g_cur, g_prev = gate_cols(gate_ref[rows, :], pos)
                d_out = (g_cur * dy_ref[rows, :].astype(jnp.float32)).astype(jnp.bfloat16)
                _, d_one, d_three = hidden_grads(x_ref[rows, :], d_out, b_one[slot], b_three[slot], b_two[slot])
                dx = (dot_nt(d_one.astype(jnp.bfloat16), b_one[slot]) + dot_nt(d_three.astype(jnp.bfloat16), b_three[slot])).astype(jnp.bfloat16)
                acc = dx_ref[rows, :]
                both = (acc.astype(jnp.float32) + dx.astype(jnp.float32)).astype(jnp.bfloat16)
                dx_ref[rows, :] = jnp.where(g_cur > 0, jnp.where(g_prev > 0, both, dx), acc)
            return 0

        return lax.fori_loop(0, n_tile, tile, 0)

    lax.fori_loop(0, n_pos, expert, 0)


def dw_kernel(n_src, has_acc, last, cnt_ref, list_ref, gate_ref, *refs):
    refs = list(refs)
    x_refs = [refs.pop(0) for _ in range(n_src)]
    dy_refs = [refs.pop(0) for _ in range(n_src)]
    w_one, w_three, w_two = [refs.pop(0) for _ in range(3)]
    acc_in = [refs.pop(0) for _ in range(3)] if has_acc else None
    outs = [refs.pop(0) for _ in range(3)]
    acc = [refs.pop(0) for _ in range(3)]
    x_buf, dy_buf, t_sems, a_sems = refs[:4]
    stage_bufs = refs[4:]
    q = pl.program_id(0)
    n_tile = gate_ref.shape[0] // TILE
    n_act = cnt_ref[q]

    def start(step, slot):
        tid = list_ref[q, step]
        row = pl.ds(pl.multiple_of(lax.rem(tid, n_tile) * TILE, TILE), TILE)
        for k in range(n_src):
            @pl.when(tid // n_tile == k)
            def _():
                pltpu.make_async_copy(x_refs[k].at[row, :], x_buf.at[slot], t_sems.at[slot, 0]).start()
                pltpu.make_async_copy(dy_refs[k].at[row, :], dy_buf.at[slot], t_sems.at[slot, 1]).start()

    @pl.when(n_act > 0)
    def _():
        start(0, 0)

    if has_acc:
        copies = [pltpu.make_async_copy(acc_in[mat].at[q], acc[mat], a_sems.at[mat]) for mat in range(3)]
        for copy in copies:
            copy.start()
        for copy in copies:
            copy.wait()
    else:
        for mat in range(3):
            acc[mat][...] = jnp.zeros_like(acc[mat])

    def body(step, _):
        slot = lax.rem(step, 2)
        tid = list_ref[q, step]
        pltpu.make_async_copy(x_refs[0].at[pl.ds(0, TILE), :], x_buf.at[slot], t_sems.at[slot, 0]).wait()
        pltpu.make_async_copy(dy_refs[0].at[pl.ds(0, TILE), :], dy_buf.at[slot], t_sems.at[slot, 1]).wait()

        @pl.when(step + 1 < n_act)
        def _():
            start(step + 1, 1 - slot)

        gates = gate_ref[pl.ds(pl.multiple_of(lax.rem(tid, n_tile) * TILE, TILE), TILE), :]
        g_cur, _ = gate_cols(gates, (tid // n_tile) * 2 + q)
        chosen = g_cur > 0
        x = x_buf[slot]
        d_out = (g_cur * dy_buf[slot].astype(jnp.float32)).astype(jnp.bfloat16)
        hidden, d_one, d_three = hidden_grads(x, d_out, w_one[0], w_three[0], w_two[0])
        hidden = jnp.where(chosen, hidden, 0.0).astype(jnp.bfloat16)
        d_one = jnp.where(chosen, d_one, 0.0).astype(jnp.bfloat16)
        d_three = jnp.where(chosen, d_three, 0.0).astype(jnp.bfloat16)
        acc[0][...] += dot_tn(x, d_one)
        acc[1][...] += dot_tn(x, d_three)
        acc[2][...] += dot_tn(hidden, d_out)
        return 0

    lax.fori_loop(0, n_act, body, 0)

    copies = []
    for mat in range(3):
        src = acc[mat]
        if last:
            src = stage_bufs[mat]
            src[...] = acc[mat][...].astype(jnp.bfloat16)
        copies.append(pltpu.make_async_copy(src, outs[mat].at[q], a_sems.at[mat]))
        copies[-1].start()
    for copy in copies:
        copy.wait()


ANY = pl.BlockSpec(memory_space=pl.ANY)
SMEM = pl.BlockSpec(memory_space=pltpu.SMEM)
VMEM = pl.BlockSpec(memory_space=pltpu.VMEM)


def params():
    return pltpu.CompilerParams(vmem_limit_bytes=VMEM_BYTES)


def weight_bufs(w_one, w_two):
    return [
        pltpu.VMEM((2,) + w_one.shape[1:], jnp.bfloat16),
        pltpu.VMEM((2,) + w_one.shape[1:], jnp.bfloat16),
        pltpu.VMEM((2,) + w_two.shape[1:], jnp.bfloat16),
        pltpu.SemaphoreType.DMA((2, 3)),
    ]


def run_fwd(act, gates, x, groups):
    n_tok, d = x.shape
    f = groups[0][0].shape[2]
    w_flat = [m for g in groups for m in g]
    return pl.pallas_call(
        functools.partial(fwd_kernel, len(groups)),
        out_shape=jax.ShapeDtypeStruct((n_tok, d), jnp.bfloat16),
        in_specs=[SMEM, VMEM, VMEM] + [ANY] * len(w_flat),
        out_specs=VMEM,
        scratch_shapes=weight_bufs(groups[0][0], groups[0][2]),
        compiler_params=params(),
        cost_estimate=pl.CostEstimate(flops=2 * 3 * 2 * n_tok * d * f, bytes_accessed=100_000_000, transcendentals=0),
        name="fwd_tiles",
    )(act, gates, x, *w_flat)


def run_dx(act, gates, x, dy, groups):
    n_tok, d = x.shape
    f = groups[0][0].shape[2]
    w_flat = [m for g in groups for m in g]
    return pl.pallas_call(
        functools.partial(dx_kernel, len(groups)),
        out_shape=jax.ShapeDtypeStruct((n_tok, d), jnp.bfloat16),
        in_specs=[SMEM, VMEM, VMEM, VMEM] + [ANY] * len(w_flat),
        out_specs=VMEM,
        scratch_shapes=weight_bufs(groups[0][0], groups[0][2]),
        compiler_params=params(),
        cost_estimate=pl.CostEstimate(flops=2 * 5 * 2 * n_tok * d * f, bytes_accessed=100_000_000, transcendentals=0),
        name="dx_tiles",
    )(act, gates, x, dy, *w_flat)


def run_dw(cnt, tiles, gates, xs, dys, weights, acc, last):
    d, f = weights[0].shape[1:]
    n_src = len(xs)
    n_local = weights[0].shape[0]
    shapes = [(d, f), (d, f), (f, d)]
    out_dtype = jnp.bfloat16 if last else jnp.float32
    w_specs = [pl.BlockSpec((1,) + s, lambda q: (q, 0, 0)) for s in shapes]
    return pl.pallas_call(
        functools.partial(dw_kernel, n_src, acc is not None, last),
        grid=(n_local,),
        out_shape=[jax.ShapeDtypeStruct((n_local,) + s, out_dtype) for s in shapes],
        in_specs=[SMEM, SMEM, pl.BlockSpec(gates.shape, lambda q: (0, 0))] + [ANY] * (2 * n_src) + w_specs + [ANY] * (3 if acc is not None else 0),
        out_specs=[ANY] * 3,
        scratch_shapes=[pltpu.VMEM(s, jnp.float32) for s in shapes] + [
            pltpu.VMEM((2, TILE, d), jnp.bfloat16),
            pltpu.VMEM((2, TILE, d), jnp.bfloat16),
            pltpu.SemaphoreType.DMA((2, 2)),
            pltpu.SemaphoreType.DMA((3,)),
        ] + ([pltpu.VMEM(s, jnp.bfloat16) for s in shapes] if last else []),
        compiler_params=params(),
        cost_estimate=pl.CostEstimate(flops=2 * 6 * n_src * xs[0].shape[0] * d * f, bytes_accessed=100_000_000, transcendentals=0),
        name="dw_tiles",
    )(cnt, tiles, gates, *xs, *dys, *weights, *(acc or ()))


def sort_rows(rank, rows):
    n = rank.shape[0]
    pick = (lax.broadcasted_iota(jnp.int32, (n, n), 0) == rank[None, :]).astype(jnp.bfloat16)
    return jnp.dot(pick, rows, preferred_element_type=jnp.float32).astype(jnp.bfloat16)


def unsort_rows(rank, rows):
    n = rank.shape[0]
    pick = (lax.broadcasted_iota(jnp.int32, (n, n), 1) == rank[:, None]).astype(jnp.bfloat16)
    return jnp.dot(pick, rows, preferred_element_type=jnp.float32).astype(jnp.bfloat16)


def solution(mesh):
    n_stage = mesh.shape['stage']
    n_dev = mesh.shape['expert']
    to_next = [(k, (k + 1) % n_stage) for k in range(n_stage)]
    to_prev = [((k + 1) % n_stage, k) for k in range(n_stage)]
    cross = [(k, k ^ 2) for k in range(n_dev)]
    core = [(k, k ^ 1) for k in range(n_dev)]
    tok_spec = P('stage', 'expert', None)
    w_spec = P('stage', 'expert', None, None)

    def moe_layer(x_act, route_idx, route_wts, w_one, w_three, w_two, dy_act):
        x_src = x_act[0]
        n_tok, d = x_src.shape
        n_local = w_one.shape[1]
        n_exp = n_local * n_dev
        n_tile = n_tok // TILE
        me = lax.axis_index('expert')

        w_own = (w_one[0], w_three[0], w_two[0])
        w_x = tuple(lax.ppermute(w, 'expert', cross) for w in w_own)
        w_c = tuple(lax.ppermute(w, 'expert', core) for w in w_own)
        w_d = tuple(lax.ppermute(w, 'expert', core) for w in w_x)

        idx = route_idx[0]
        lo, hi = jnp.min(idx, axis=1), jnp.max(idx, axis=1)
        tok_ids = jnp.arange(n_tok, dtype=jnp.int32)
        key = (lo * n_exp + hi) * n_tok + tok_ids
        rank = jnp.sum((key[None, :] < key[:, None]).astype(jnp.int32), axis=1)
        hit = lax.broadcasted_iota(jnp.int32, (n_tok, n_tok), 0) == rank[None, :]
        cols = [idx[:, 0].astype(jnp.float32), idx[:, 1].astype(jnp.float32), route_wts[0][:, 0], route_wts[0][:, 1]]
        meta = [jnp.sum(jnp.where(hit, c[None, :], 0.0), axis=1) for c in cols] + [rank.astype(jnp.float32)]
        meta = jnp.stack(meta + [jnp.zeros_like(meta[0])] * 3)
        meta = lax.ppermute(meta, 'stage', to_next)
        metas = lax.all_gather(meta, 'expert')
        rank_own = meta[4].astype(jnp.int32)

        xs = sort_rows(rank, x_src)
        x_fwd = lax.ppermute(xs, 'stage', to_next)
        xs_again, _ = lax.optimization_barrier((xs, meta))
        x_bwd = lax.ppermute(xs_again, 'stage', to_next)

        dys = sort_rows(rank_own, dy_act[0])
        dy_c = lax.ppermute(dys, 'expert', core)
        dy_x = lax.ppermute(dys, 'expert', cross)
        dy_d = lax.ppermute(dy_x, 'expert', core)
        x_c = lax.ppermute(x_bwd, 'expert', core)
        x_x = lax.ppermute(x_bwd, 'expert', cross)
        x_d = lax.ppermute(x_x, 'expert', core)

        def gates_of(tab, expert_ids):
            e_first, e_second = tab[0].astype(jnp.int32)[:, None], tab[1].astype(jnp.int32)[:, None]
            return jnp.where(e_first == expert_ids, tab[2][:, None], 0.0) + jnp.where(e_second == expert_ids, tab[3][:, None], 0.0)

        lane = jnp.arange(LANES, dtype=jnp.int32)
        pos_exp = jnp.where(lane < n_exp, n_local * jnp.bitwise_xor(me, lane // n_local) + lane % n_local, -1)[None, :]
        gates = gates_of(meta, pos_exp)
        act = (jnp.max(gates[:, :n_exp].reshape(n_tile, TILE, n_exp), axis=1) > 0).astype(jnp.int32).T.reshape(-1)

        src_order = [jnp.bitwise_xor(me, k) for k in range(n_dev)]
        own_exp = n_local * me + jnp.arange(n_local, dtype=jnp.int32)[None, :]
        gates_all = jnp.concatenate([gates_of(lax.dynamic_index_in_dim(metas, s, 0, False), own_exp) for s in src_order], axis=1)

        def tile_list(g):
            hits = (jnp.max(g.reshape(n_tile, TILE, -1, n_local), axis=1) > 0).astype(jnp.int32)
            hits = jnp.transpose(hits, (2, 1, 0)).reshape(n_local, -1)
            place = jnp.cumsum(hits, axis=1) - 1
            n = hits.shape[1]
            ids = jnp.arange(n, dtype=jnp.int32)
            sel = (place[:, None, :] == ids[None, :, None]) & (hits[:, None, :] > 0)
            return jnp.sum(hits, axis=1), jnp.sum(jnp.where(sel, ids[None, None, :], 0), axis=2)

        def pad_lanes(g):
            return jnp.pad(g, ((0, 0), (0, LANES - g.shape[1])))

        near, far = gates_all[:, :2 * n_local], gates_all[:, 2 * n_local:]
        cnt_near, list_near = tile_list(near)
        cnt_far, list_far = tile_list(far)

        groups = (w_own, w_c, w_x, w_d)
        acc = run_dw(cnt_near, list_near, pad_lanes(near), (x_bwd, x_c), (dys, dy_c), w_own, None, False)
        dxs = run_dx(act, gates, x_bwd, dys, groups)
        dx_back = lax.ppermute(dxs, 'stage', to_prev)
        ys = run_fwd(act, gates, x_fwd, groups)
        y_own = unsort_rows(rank_own, ys)
        g_one, g_three, g_two = run_dw(cnt_far, list_far, pad_lanes(far), (x_x, x_d), (dy_x, dy_d), w_own, tuple(acc), True)
        dx_own = unsort_rows(rank, dx_back)
        return y_own[None], dx_own[None], g_one[None], g_three[None], g_two[None]

    return jax.shard_map(moe_layer, mesh=mesh, in_specs=(tok_spec, tok_spec, tok_spec, w_spec, w_spec, w_spec, tok_spec), out_specs=(tok_spec, tok_spec, w_spec, w_spec, w_spec), check_vma=False)
```

time: 3450 us -> 1120 us (0.32)
  the two profiles are of different devices: /device:TPU:0 before, /device:TPU:4 now
where the time goes in v1:
time: 1120 us; the launch traced here: 1110 us
  waiting for transfers between devices  407 us (36%)
  Pallas kernels  401 us (36%)
  blocking collectives  184 us (16%)
  matrix products  84.7 us (8%)
  other arithmetic  17.7 us (2%)
    ppermute x3, waiting for transfers between devices, moe_layer(): w_x = tuple((lax.ppermute(w, 'expert', cross) for w in w_own))  347 us
    pallas_call x2, Pallas kernels, run_dw(): pl.pallas_call(functools.partial(dw_kernel, n_src, acc is not None, last)...  215 us
    all_gather x1, blocking collectives, moe_layer(): metas = lax.all_gather(meta, 'expert')  184 us
    pallas_call x1, Pallas kernels, run_dx(): pl.pallas_call(functools.partial(dx_kernel, len(groups)), out_shape=jax.S...  115 us
    pallas_call x1, Pallas kernels, run_fwd(): pl.pallas_call(functools.partial(fwd_kernel, len(groups)), out_shape=jax....  71 us
    ppermute x1, waiting for transfers between devices, moe_layer(): x_fwd = lax.ppermute(xs, 'stage', to_next)  58.1 us
    dot_general x2, matrix products, unsort_rows(): jnp.dot(pick, rows, preferred_element_type=jnp.float32).astype(jnp.bfloat16)  44.3 us
    dot_general x2, matrix products, sort_rows(): jnp.dot(pick, rows, preferred_element_type=jnp.float32).astype(jnp.bfloat16)  40.4 us
  transfers between devices with their start and end apart: 19, of which 5 were waited for; matrix products, arithmetic and copies ran while one was open for 10% of the time, Pallas kernels for 26%

profile of v1, /device:TPU:4, one launch (start us, length us, event | category | flops | bytes accessed | tf_op | source)
XLA Modules:
  0.0 1108.5 jit_solution(15732377704432221183)
XLA Ops:
  0.6 1.5 collective-permute-start.7
  2.1 0.5 collective-permute-start.5
  2.7 0.8 fusion.29
  3.5 1.8 convert_reduce_fusion
  5.3 0.0 copy-start.1
  5.3 0.8 slice_convert_fusion.4
  6.1 0.8 fusion.30
  6.9 9.4 select_reduce_fusion
  16.4 0.1 stack.24
  16.5 0.0 collective-permute-start
  16.5 0.0 collective-permute-start.2
  16.5 0.0 slice-start
  16.6 0.0 slice-start.1
  16.6 1.9 collective-permute-start.6
  18.5 2.3 collective-permute-done
  20.8 0.0 collective-permute-start.3
  20.8 118.6 %collective-permute-done.7.refs_8_ = bf16[2,768,2048]{2,1,0:T(8,128)(2,1)} collective-permute-done((bf16[2,768,2048]{2,1,0:T(8,128)(2,1)}, bf16[2,768,2048]{2,1,0:T(8,128)(2,1)}, u32[]{:S(2)}, u32[]{:S(2)}) %collective-permute-start.7) | collective-permute-done | bytes 6291488 | tf_op jit(solution)/shard_map/ppermute | solution.py:318
  139.4 21.0 %fusion.13 = bf16[2048,2048]{1,0:T(8,128)(2,1)} fusion(bf16[1,2048,2048]{2,1,0:T(8,128)(2,1)} %param.7, s32[2048]{0:T(1024)S(1)} %convert_reduce_fusion), kind=kOutput, calls=%fused_computation.22 | convolution fusion | flops 17188257792 | bytes 16785408 | tf_op jit(solution)/shard_map/dot_general | solution.py:290
  160.4 113.8 %collective-permute-done.5.refs_6_ = bf16[2,2048,768]{2,1,0:T(8,128)(2,1)} collective-permute-done((bf16[2,2048,768]{2,1,0:T(8,128)(2,1)}, bf16[2,2048,768]{2,1,0:T(8,128)(2,1)}, u32[]{:S(2)}, u32[]{:S(2)}) %collective-permute-start.5) | collective-permute-done | bytes 6291488 | tf_op jit(solution)/shard_map/ppermute | solution.py:318
  274.2 0.0 collective-permute-start.11
  274.2 19.4 %fusion.10.dy_ref.refs_2_ = bf16[2048,2048]{1,0:T(8,128)(2,1)} fusion(bf16[1,2048,2048]{2,1,0:T(8,128)(2,1)S(1)} %bitcast.112, s32[2048]{0:T(1024)S(1)} %bitcast.101), kind=kOutput, calls=%fused_computation.21 | convolution fusion | flops 17188257792 | bytes 16785408 | tf_op jit(solution)/shard_map/dot_general | solution.py:290
  293.6 114.3 %collective-permute-done.6.refs_7_ = bf16[2,2048,768]{2,1,0:T(8,128)(2,1)} collective-permute-done((bf16[2,2048,768]{2,1,0:T(8,128)(2,1)}, bf16[2,2048,768]{2,1,0:T(8,128)(2,1)}, u32[]{:S(2)}, u32[]{:S(2)}) %collective-permute-start.6) | collective-permute-done | bytes 6291488 | tf_op jit(solution)/shard_map/ppermute | solution.py:318
  407.9 1.5 collective-permute-start.15
  409.4 0.0 collective-permute-done.2.refs_3_
  409.4 0.5 collective-permute-start.8
  409.9 0.0 collective-permute-done.4.refs_5_
  409.9 0.0 collective-permute-start.9
  409.9 184.3 %all-gather = f32[32,2048]{1,0:T(8,128)S(1)} all-gather(f32[8,2048]{1,0:T(8,128)S(1)} %collective-permute-done), channel_id=2, replica_groups=mesh['stage'=2,'expert'=4] {'expert'}, dimensions={0}, use_global_device_ids=true | all-gather | bytes 327680 | tf_op jit(solution)/shard_map/all_gather | solution.py:332
  594.2 0.1 dynamic-slice_convert_fusion.3
  594.3 0.1 fusion.18
  594.5 0.4 copy.23
  594.9 0.1 reduce_max.39
  595.0 0.1 reduce_window_sum.23
  595.1 0.2 reduce_window_sum.24
  595.3 1.0 pad.8.gate_ref
  596.3 0.4 copy.21
  596.7 0.1 reduce_max.38
  596.8 0.0 collective-permute-done.11.x_ref.refs_0_
  596.8 0.2 collective-permute-start.1
  597.0 0.1 reduce_window_sum.21
  597.1 0.2 reduce_window_sum.22
  597.3 1.1 pad.7.gate_ref
  598.4 1.1 select_add_fusion.gate_ref
  599.6 0.0 copy-start
  599.6 0.1 bitcast_reduce_fusion
  599.7 0.1 copy.19
  599.8 0.7 reshape.247.act_ref
  600.4 0.7 fusion.25.cnt_ref
  601.1 0.7 fusion.23.cnt_ref
  601.8 0.7 select_reduce_fusion.4.list_ref
  602.5 0.7 select_reduce_fusion.5.list_ref
  603.2 0.0 collective-permute-done.15.refs_2_
  603.2 0.5 collective-permute-start.17
  603.7 0.0 collective-permute-done.8.refs_9_
  603.8 0.5 collective-permute-start.13
  604.2 0.0 collective-permute-done.9.refs_10_
  604.3 115.0 %dx_tiles.1 = bf16[2048,2048]{1,0:T(8,128)(2,1)} custom-call(s32[64]{0:T(128)} %reshape.247.act_ref, f32[2048,128]{1,0:T(8,128)} %copy-done, bf16[2048,2048]{1,0:T(8,128)(2,1)} %collective-permute-done.11.x_ref.refs_0_, bf16[2048,2048]{1,0:T(8,128)(2,1)} %fusion.10.dy_ref.refs_2_, bf16[2,2048,768]{2,1,0:T(8,128)(2,1)} %bitcast.115, ...), custom_call_target="tpu_custom_call" | custom-call | flops 64424509440 | bytes 100000000 | tf_op jit(solution)/shard_map/dx_tiles/pallas_call | solution.py:250
  719.3 58.1 %collective-permute-done.1.x_ref = bf16[2048,2048]{1,0:T(8,128)(2,1)} collective-permute-done((bf16[2048,2048]{1,0:T(8,128)(2,1)}, bf16[2048,2048]{1,0:T(8,128)(2,1)}, u32[]{:S(2)}, u32[]{:S(2)}) %collective-permute-start.1) | collective-permute-done | bytes 8388640 | tf_op jit(solution)/shard_map/ppermute | solution.py:336
  777.4 0.2 collective-permute-start.12
  777.6 71.0 %fwd_tiles.1 = bf16[2048,2048]{1,0:T(8,128)(2,1)} custom-call(s32[64]{0:T(128)} %reshape.247.act_ref, f32[2048,128]{1,0:T(8,128)} %copy-done, bf16[2048,2048]{1,0:T(8,128)(2,1)} %collective-permute-done.1.x_ref, bf16[2,2048,768]{2,1,0:T(8,128)(2,1)} %bitcast.116, bf16[2,2048,768]{2,1,0:T(8,128)(2,1)} %bitcast.122, bf16[2,768,2048]{2,1,0:T(8,128)(2,1)} %bitcast.128, ...), custom_call_target="tpu_custom_call" | custom-call | flops 38654705664 | bytes 100000000 | tf_op jit(solution)/shard_map/fwd_tiles/pallas_call | solution.py:234
  848.6 22.1 %convert_bitcast_fusion.1 = bf16[1,2048,2048]{2,1,0:T(8,128)(2,1)} fusion(bf16[2048,2048]{1,0:T(8,128)(2,1)} %fwd_tiles.1, s32[2048]{0:T(1024)S(1)} %bitcast.102), kind=kOutput, calls=%fused_computation.18 | convolution fusion | flops 17188257792 | bytes 16785408 | tf_op jit(solution)/shard_map/dot_general | solution.py:296
  870.8 104.6 %dw_tiles.2 = (f32[2,2048,768]{2,1,0:T(8,128)}, f32[2,2048,768]{2,1,0:T(8,128)}, f32[2,768,2048]{2,1,0:T(8,128)}) custom-call(s32[2]{0:T(128)} %fusion.25.cnt_ref, s32[2,16]{1,0:T(2,128)} %select_reduce_fusion.4.list_ref, f32[2048,128]{1,0:T(8,128)} %pad.8.gate_ref, bf16[2048,2048]{1,0:T(8,128)(2,1)} %collective-permute-done.11.x_ref.refs_0_, ...), custom_call_target="tpu_custom_call" | custom-call | flops 77309411328 | bytes 100000000 | tf_op jit(solution)/shard_map/dw_tiles/pallas_call | solution.py:269
  975.4 22.1 %convert_bitcast_fusion = bf16[1,2048,2048]{2,1,0:T(8,128)(2,1)} fusion(bf16[2048,2048]{1,0:T(8,128)(2,1)} %collective-permute-done.12, s32[2048]{0:T(1024)S(1)} %copy-done.2), kind=kOutput, calls=%fused_computation.15 | convolution fusion | flops 17188257792 | bytes 16785408 | tf_op jit(solution)/shard_map/dot_general | solution.py:296
  997.5 110.5 %dw_tiles.3 = (bf16[2,2048,768]{2,1,0:T(8,128)(2,1)}, bf16[2,2048,768]{2,1,0:T(8,128)(2,1)}, bf16[2,768,2048]{2,1,0:T(8,128)(2,1)}) custom-call(s32[2]{0:T(128)} %fusion.23.cnt_ref, s32[2,16]{1,0:T(2,128)} %select_reduce_fusion.5.list_ref, f32[2048,128]{1,0:T(8,128)} %pad.7.gate_ref, bf16[2048,2048]{1,0:T(8,128)(2,1)} %collective-permute-done.13.refs_0_, ...), custom_call_target="tpu_custom_call" | custom-call | flops 77309411328 | bytes 100000000 | tf_op jit(solution)/shard_map/dw_tiles/pallas_call | solution.py:269
  (39 shorter events, 0.2 us)
Async XLA Ops:
  0.6 138.7 %collective-permute-start.7 = (bf16[2,768,2048]{2,1,0:T(8,128)(2,1)}, bf16[2,768,2048]{2,1,0:T(8,128)(2,1)}, u32[]{:S(2)}, u32[]{:S(2)}) collective-permute-start(bf16[2,768,2048]{2,1,0:T(8,128)(2,1)} %bitcast.125), channel_id=1, source_target_pairs={{0,2},{1,3},{2,0},{3,1},{4,6},{5,7},{6,4},{7,5}} | collective-permute-start | bytes 18874376 | tf_op jit(solution)/shard_map/ppermute | solution.py:318
  2.1 272.0 %collective-permute-start.5 = (bf16[2,2048,768]{2,1,0:T(8,128)(2,1)}, bf16[2,2048,768]{2,1,0:T(8,128)(2,1)}, u32[]{:S(2)}, u32[]{:S(2)}) collective-permute-start(bf16[2,2048,768]{2,1,0:T(8,128)(2,1)} %bitcast.113), channel_id=1, source_target_pairs={{0,2},{1,3},{2,0},{3,1},{4,6},{5,7},{6,4},{7,5}} | collective-permute-start | bytes 18874376 | tf_op jit(solution)/shard_map/ppermute | solution.py:318
  5.3 155.1 %copy-start.1 = (s32[2048]{0:T(1024)}, s32[2048]{0:T(1024)S(1)}, u32[]{:S(2)}) copy-start(s32[2048]{0:T(1024)S(1)} %convert_reduce_fusion) | copy-start | bytes 24580
  16.5 4.3 collective-permute-start
  16.5 392.9 %collective-permute-start.2 = (bf16[2,2048,768]{2,1,0:T(8,128)(2,1)}, bf16[2,2048,768]{2,1,0:T(8,128)(2,1)}, u32[]{:S(2)}, u32[]{:S(2)}) collective-permute-start(bf16[2,2048,768]{2,1,0:T(8,128)(2,1)} %bitcast.114), channel_id=1, source_target_pairs={{0,1},{1,0},{2,3},{3,2},{4,5},{5,4},{6,7},{7,6}} | collective-permute-start | bytes 18874376 | tf_op jit(solution)/shard_map/ppermute | solution.py:319
  16.5 257.6 %slice-start = ((s8[8388608]{0:T(1024)(128)(4,1)}), s8[4194304]{0:T(1024)(128)(4,1)S(1)}, s32[]{:S(2)}) async-start(s8[8388608]{0:T(1024)(128)(4,1)} %bitcast.111), calls=%async_computation | async-start | bytes 8388608
  16.6 257.6 %slice-start.1 = ((s8[8388608]{0:T(1024)(128)(4,1)}), s8[4194304]{0:T(1024)(128)(4,1)S(1)}, s32[]{:S(2)}) async-start(s8[8388608]{0:T(1024)(128)(4,1)} %bitcast.111), calls=%async_computation.1 | async-start | bytes 8388608
  16.6 391.3 %collective-permute-start.6 = (bf16[2,2048,768]{2,1,0:T(8,128)(2,1)}, bf16[2,2048,768]{2,1,0:T(8,128)(2,1)}, u32[]{:S(2)}, u32[]{:S(2)}) collective-permute-start(bf16[2,2048,768]{2,1,0:T(8,128)(2,1)} %bitcast.119), channel_id=1, source_target_pairs={{0,2},{1,3},{2,0},{3,1},{4,6},{5,7},{6,4},{7,5}} | collective-permute-start | bytes 18874376 | tf_op jit(solution)/shard_map/ppermute | solution.py:318
  20.8 388.6 %collective-permute-start.3 = (bf16[2,2048,768]{2,1,0:T(8,128)(2,1)}, bf16[2,2048,768]{2,1,0:T(8,128)(2,1)}, u32[]{:S(2)}, u32[]{:S(2)}) collective-permute-start(bf16[2,2048,768]{2,1,0:T(8,128)(2,1)} %bitcast.120), channel_id=1, source_target_pairs={{0,1},{1,0},{2,3},{3,2},{4,5},{5,4},{6,7},{7,6}} | collective-permute-start | bytes 18874376 | tf_op jit(solution)/shard_map/ppermute | solution.py:319
  139.4 270.5 %collective-permute-start.4 = (bf16[2,768,2048]{2,1,0:T(8,128)(2,1)}, bf16[2,768,2048]{2,1,0:T(8,128)(2,1)}, u32[]{:S(2)}, u32[]{:S(2)}) collective-permute-start(bf16[2,768,2048]{2,1,0:T(8,128)(2,1)} %bitcast.126), channel_id=1, source_target_pairs={{0,1},{1,0},{2,3},{3,2},{4,5},{5,4},{6,7},{7,6}} | collective-permute-start | bytes 18874376 | tf_op jit(solution)/shard_map/ppermute | solution.py:319
  274.2 322.6 %collective-permute-start.11 = (bf16[2048,2048]{1,0:T(8,128)(2,1)}, bf16[2048,2048]{1,0:T(8,128)(2,1)}, u32[]{:S(2)}, u32[]{:S(2)}) collective-permute-start(bf16[2048,2048]{1,0:T(8,128)(2,1)} %fusion.13), channel_id=1, source_target_pairs={{0,4},{4,0},{1,5},{5,1},{2,6},{6,2},{3,7},{7,3}} | collective-permute-start | bytes 25165832 | tf_op jit(solution)/shard_map/ppermute | solution.py:338
  407.9 195.4 %collective-permute-start.15 = (bf16[2048,2048]{1,0:T(8,128)(2,1)}, bf16[2048,2048]{1,0:T(8,128)(2,1)}, u32[]{:S(2)}, u32[]{:S(2)}) collective-permute-start(bf16[2048,2048]{1,0:T(8,128)(2,1)} %fusion.10.dy_ref.refs_2_), channel_id=1, source_target_pairs={{0,2},{1,3},{2,0},{3,1},{4,6},{5,7},{6,4},{7,5}} | collective-permute-start | bytes 25165832 | tf_op jit(solution)/shard_map/ppermute | solution.py:342
  409.4 193.9 %collective-permute-start.10 = (bf16[2,768,2048]{2,1,0:T(8,128)(2,1)}, bf16[2,768,2048]{2,1,0:T(8,128)(2,1)}, u32[]{:S(2)}, u32[]{:S(2)}) collective-permute-start(bf16[2,768,2048]{2,1,0:T(8,128)(2,1)} %collective-permute-done.7.refs_8_), channel_id=1, source_target_pairs={{0,1},{1,0},{2,3},{3,2},{4,5},{5,4},{6,7},{7,6}} | collective-permute-start | bytes 18874376 | tf_op jit(solution)/shard_map/ppermute | solution.py:320
  409.4 194.4 %collective-permute-start.8 = (bf16[2,2048,768]{2,1,0:T(8,128)(2,1)}, bf16[2,2048,768]{2,1,0:T(8,128)(2,1)}, u32[]{:S(2)}, u32[]{:S(2)}) collective-permute-start(bf16[2,2048,768]{2,1,0:T(8,128)(2,1)} %collective-permute-done.5.refs_6_), channel_id=1, source_target_pairs={{0,1},{1,0},{2,3},{3,2},{4,5},{5,4},{6,7},{7,6}} | collective-permute-start | bytes 18874376 | tf_op jit(solution)/shard_map/ppermute | solution.py:320
  409.9 194.4 %collective-permute-start.9 = (bf16[2,2048,768]{2,1,0:T(8,128)(2,1)}, bf16[2,2048,768]{2,1,0:T(8,128)(2,1)}, u32[]{:S(2)}, u32[]{:S(2)}) collective-permute-start(bf16[2,2048,768]{2,1,0:T(8,128)(2,1)} %collective-permute-done.6.refs_7_), channel_id=1, source_target_pairs={{0,1},{1,0},{2,3},{3,2},{4,5},{5,4},{6,7},{7,6}} | collective-permute-start | bytes 18874376 | tf_op jit(solution)/shard_map/ppermute | solution.py:320
  596.8 180.6 %collective-permute-start.1 = (bf16[2048,2048]{1,0:T(8,128)(2,1)}, bf16[2048,2048]{1,0:T(8,128)(2,1)}, u32[]{:S(2)}, u32[]{:S(2)}) collective-permute-start(bf16[2048,2048]{1,0:T(8,128)(2,1)} %fusion.13), channel_id=1, source_target_pairs={{0,4},{4,0},{1,5},{5,1},{2,6},{6,2},{3,7},{7,3}} | collective-permute-start | bytes 25165832 | tf_op jit(solution)/shard_map/ppermute | solution.py:336
  599.6 4.7 copy-start
  603.2 267.5 %collective-permute-start.18 = (bf16[2048,2048]{1,0:T(8,128)(2,1)}, bf16[2048,2048]{1,0:T(8,128)(2,1)}, u32[]{:S(2)}, u32[]{:S(2)}) collective-permute-start(bf16[2048,2048]{1,0:T(8,128)(2,1)} %fusion.10.dy_ref.refs_2_), channel_id=1, source_target_pairs={{0,1},{1,0},{2,3},{3,2},{4,5},{5,4},{6,7},{7,6}} | collective-permute-start | bytes 25165832 | tf_op jit(solution)/shard_map/ppermute | solution.py:341
  603.2 267.5 %collective-permute-start.17 = (bf16[2048,2048]{1,0:T(8,128)(2,1)}, bf16[2048,2048]{1,0:T(8,128)(2,1)}, u32[]{:S(2)}, u32[]{:S(2)}) collective-permute-start(bf16[2048,2048]{1,0:T(8,128)(2,1)} %collective-permute-done.11.x_ref.refs_0_), channel_id=1, source_target_pairs={{0,1},{1,0},{2,3},{3,2},{4,5},{5,4},{6,7},{7,6}} | collective-permute-start | bytes 25165832 | tf_op jit(solution)/shard_map/ppermute | solution.py:344
  603.8 267.0 %collective-permute-start.13 = (bf16[2048,2048]{1,0:T(8,128)(2,1)}, bf16[2048,2048]{1,0:T(8,128)(2,1)}, u32[]{:S(2)}, u32[]{:S(2)}) collective-permute-start(bf16[2048,2048]{1,0:T(8,128)(2,1)} %collective-permute-done.11.x_ref.refs_0_), channel_id=1, source_target_pairs={{0,2},{1,3},{2,0},{3,1},{4,6},{5,7},{6,4},{7,5}} | collective-permute-start | bytes 25165832 | tf_op jit(solution)/shard_map/ppermute | solution.py:345
  604.3 393.3 %collective-permute-start.16 = (bf16[2048,2048]{1,0:T(8,128)(2,1)}, bf16[2048,2048]{1,0:T(8,128)(2,1)}, u32[]{:S(2)}, u32[]{:S(2)}) collective-permute-start(bf16[2048,2048]{1,0:T(8,128)(2,1)} %collective-permute-done.15.refs_2_), channel_id=1, source_target_pairs={{0,1},{1,0},{2,3},{3,2},{4,5},{5,4},{6,7},{7,6}} | collective-permute-start | bytes 25165832 | tf_op jit(solution)/shard_map/ppermute | solution.py:343
  777.4 197.9 %collective-permute-start.12 = (bf16[2048,2048]{1,0:T(8,128)(2,1)}, bf16[2048,2048]{1,0:T(8,128)(2,1)}, u32[]{:S(2)}, u32[]{:S(2)}) collective-permute-start(bf16[2048,2048]{1,0:T(8,128)(2,1)} %dx_tiles.1), channel_id=1, source_target_pairs={{4,0},{0,4},{5,1},{1,5},{6,2},{2,6},{7,3},{3,7}} | collective-permute-start | bytes 25165832 | tf_op jit(solution)/shard_map/ppermute | solution.py:380
  870.7 104.6 %copy-start.2 = (s32[2048]{0:T(1024)S(1)}, s32[2048]{0:T(1024)}, u32[]{:S(2)}) copy-start(s32[2048]{0:T(1024)} %copy-done.1) | copy-start | bytes 24580
  870.8 126.8 %collective-permute-start.14 = (bf16[2048,2048]{1,0:T(8,128)(2,1)}, bf16[2048,2048]{1,0:T(8,128)(2,1)}, u32[]{:S(2)}, u32[]{:S(2)}) collective-permute-start(bf16[2048,2048]{1,0:T(8,128)(2,1)} %collective-permute-done.13.refs_0_), channel_id=1, source_target_pairs={{0,1},{1,0},{2,3},{3,2},{4,5},{5,4},{6,7},{7,6}} | collective-permute-start | bytes 25165832 | tf_op jit(solution)/shard_map/ppermute | solution.py:346
